TPU v7x, 32 devices: a whole 2x2x4 slice. The times are simulated.
32 devices in a mesh: dp: 4 (over y, x), tensor: 8 (over z, core).
Axes of the slice: x: 2, y: 2, z: 4, core: 2. Of those that a mesh axis runs over, the one named last changes fastest.
Arguments:
- saved_input: bfloat16 [512, 8192], P(('dp', 'tensor')), may hold values from -8 to 8
- keep_bits: int32 [512, 448], P(('dp', 'tensor')), may hold values from -2147483648 to 2147483646, as said below
- norm_gain: bfloat16 [8192], P('dp'), may hold values from 0.099609375 to 1.8984375
- gate_weight: bfloat16 [8192, 14336], P('dp', 'tensor'), may hold values from -0.0625 to 0.0625
- up_weight: bfloat16 [8192, 14336], P('dp', 'tensor'), may hold values from -0.0625 to 0.0625
- down_weight: bfloat16 [14336, 8192], P('tensor', 'dp'), may hold values from -0.046875 to 0.046875
Outputs:
- layer_out: bfloat16 [512, 8192], P('tensor', 'dp')
- row_check: float32 [512], P('tensor')
Inputs may be any that keep to these rules, and one draw needn't show every extreme that they name: `keep_bits`: bit k of word w of a token is the keep bit of hidden unit 32 w + k.
All inputs are finite; a program needn't handle non-finite values.
Results may differ from a plain program's by a relative error of at most 0.017.
Values may be sent and summed in bfloat16 or wider, within the bound.
A program may use at most 64 MiB of HBM per device.

v0:
```python
import jax
import jax.numpy as jnp
from jax import lax
from jax.sharding import PartitionSpec as P

D = 8192


def on_device(saved_input, keep_bits, norm_gain, gate_weight, up_weight, down_weight):
    tensor_width = lax.axis_size("tensor")
    dp_width = lax.axis_size("dp")
    unit_words = lax.all_to_all(keep_bits, "tensor", split_axis=1, concat_axis=0, tiled=True)
    shifts = jnp.arange(32, dtype=jnp.int32)
    keep_mask = jnp.bitwise_and(jnp.right_shift(unit_words[:, :, None], shifts[None, None, :]), 1)
    keep_mask = keep_mask.reshape(unit_words.shape[0], -1)
    keep_scale = 2.0 * keep_mask.astype(jnp.float32)
    width_units = gate_weight.shape[1]
    columns = lax.all_to_all(saved_input, "dp", split_axis=1, concat_axis=0, tiled=True)
    collected = lax.all_gather(columns, "tensor", axis=0, tiled=True)
    per_device = saved_input.shape[0]
    collected = collected.reshape(tensor_width, dp_width, per_device, collected.shape[1])
    collected = collected.transpose(1, 0, 2, 3).reshape(-1, collected.shape[3])
    widened = collected.astype(jnp.float32)
    squares = lax.psum(jnp.sum(widened * widened, axis=1), "dp")
    inv_rms = lax.rsqrt(squares / D + 1e-05)
    normed = (widened * inv_rms[:, None] * norm_gain.astype(jnp.float32)[None, :]).astype(
        jnp.bfloat16
    )
    gate_part = jnp.dot(normed, gate_weight, preferred_element_type=jnp.float32)
    up_part = jnp.dot(normed, up_weight, preferred_element_type=jnp.float32)
    projected = lax.psum_scatter(
        jnp.concatenate((gate_part, up_part), axis=1).astype(jnp.bfloat16),
        "dp",
        scatter_dimension=0,
        tiled=True,
    ).astype(jnp.float32)
    gate_sum = projected[:, :width_units]
    up_sum = projected[:, width_units:]
    hidden = (jax.nn.silu(gate_sum) * up_sum * keep_scale).astype(jnp.bfloat16)
    partial_value = jnp.dot(
        lax.all_gather(hidden, "dp", axis=0, tiled=True),
        down_weight,
        preferred_element_type=jnp.float32,
    )
    mlp_sum = lax.psum_scatter(
        partial_value.astype(jnp.bfloat16), "tensor", scatter_dimension=0, tiled=True
    ).astype(jnp.float32)
    out_rows = mlp_sum.shape[0]
    first_row = lax.axis_index("tensor") * out_rows
    residual = lax.dynamic_slice_in_dim(collected, first_row, out_rows, 0)
    layer_out = (residual.astype(jnp.float32) + mlp_sum).astype(jnp.bfloat16)
    widened_out = layer_out.astype(jnp.float32)
    row_check = lax.psum(jnp.sum(widened_out * widened_out, axis=1), "dp") / D
    return (layer_out, row_check)


def solution(mesh):
    placed = (
        P(("dp", "tensor"), None),
        P(("dp", "tensor"), None),
        P("dp"),
        P("dp", "tensor"),
        P("dp", "tensor"),
        P("tensor", "dp"),
    )
    return jax.shard_map(
        on_device,
        mesh=mesh,
        in_specs=placed,
        out_specs=(P("tensor", "dp"), P("tensor")),
        check_vma=False,
    )
```

profile of v0, /device:TPU:0, one launch (start us, length us, event | category | flops | bytes accessed | tf_op | source)
XLA Modules:
  0.0 222.7 jit_solution(6830503011668420196)
XLA Ops:
  7.2 0.0 all-gather.3.cloned.1.call-start
  7.2 1.0 copy.31
  8.2 10.8 %all_to_all.35 = bf16[16,4,2048]{2,0,1:T(8,128)(2,1)} all-to-all(bf16[16,4,2048]{2,0,1:T(8,128)(2,1)S(1)} %bitcast.30), channel_id=1, replica_groups=mesh['dp'=4,'tensor'=8] {'dp'}, dimensions={1} | all-to-all | bytes 524288 | tf_op jit(solution)/shard_map/all_to_all | solution.py:18
  19.0 0.0 all-gather.3.cloned.1.call-update
  19.0 0.0 reduce-scatter.3.cloned.1.call-start
  19.1 0.7 convert_element_type.40
  19.8 28.3 %all-gather.3.cloned.1.call-done = bf16[512,2048]{1,0:T(8,128)(2,1)} async-done(((bf16[64,2048]{1,0:T(8,128)(2,1)}), bf16[512,2048]{1,0:T(8,128)(2,1)}) %all-gather.3.cloned.1.call-update) | async-done | bytes 2097168 | tf_op jit(solution)/shard_map/all_gather | solution.py:19
  48.1 0.0 copy-start
  48.1 1.9 copy.23
  49.9 0.3 copy-done
  50.3 0.0 copy-start.1
  50.3 0.5 multiply_reduce_fusion
  50.8 0.1 reduce_sum.21
  50.8 9.8 %psum.14 = f32[512]{0:T(512)S(1)} all-reduce(f32[512]{0:T(512)S(1)} %reduce_sum.21), channel_id=1, replica_groups=mesh['dp'=4,'tensor'=8] {'dp'}, use_global_device_ids=true, to_apply=%region_1.0 | all-reduce | flops 512 | bytes 4096 | tf_op jit(solution)/shard_map/psum | solution.py:24
  60.7 7.1 %convolution_convert_fusion.2 = bf16[512,1792]{1,0:T(8,128)(2,1)S(1)} fusion(bf16[2048,1792]{1,0:T(8,128)(2,1)} %param.9, bf16[512,2048]{1,0:T(8,128)(2,1)S(1)} %bitcast.26, f32[2048]{0:T(1024)S(1)} %convert_element_type.40, f32[512]{0:T(512)S(1)} %add_rsqrt_fusion), kind=kOutput, calls=%fused_computation.5 | convolution fusion | flops 3763208192 | bytes 11282432 | tf_op jit(solution)/shard_map/dot_general | solution.py:29
  67.8 0.0 copy-done.1
  67.8 7.1 %convolution_convert_fusion.1 = bf16[512,1792]{1,0:T(8,128)(2,1)S(1)} fusion(bf16[2048,1792]{1,0:T(8,128)(2,1)} %param.10, bf16[512,2048]{1,0:T(8,128)(2,1)S(1)} %bitcast.27, f32[2048]{0:T(1024)S(1)} %convert_element_type.40, f32[512]{0:T(512)S(1)} %add_rsqrt_fusion), kind=kOutput, calls=%fused_computation.4 | convolution fusion | flops 3763208192 | bytes 11282432 | tf_op jit(solution)/shard_map/dot_general | solution.py:30
  74.9 2.1 pad_maximum_fusion
  77.1 0.0 copy-start.2
  77.1 0.0 reduce-scatter.3.cloned.1.call-update
  77.1 0.7 copy-done.2
  77.8 0.1 all_to_all.30
  77.9 0.7 reshape.26
  78.7 3.4 %all-to-all-start.1 = ((s32[8,1,896]{2,1,0:T(1,128)}), s32[8,1,896]{2,1,0:T(1,128)S(1)}, u32[]{:S(2)}, u32[]{:S(2)}) async-start(s32[8,1,896]{2,1,0:T(1,128)} %reshape.26), calls=%async_computation.2 | async-start | bytes 57344 | tf_op jit(solution)/shard_map/all_to_all | solution.py:12
  82.0 0.0 all-gather.5.cloned.1.call-start
  82.1 0.1 shift_right_arithmetic.26
  82.2 5.5 %all-to-all-done.1 = s32[8,1,896]{2,1,0:T(1,128)S(1)} async-done(((s32[8,1,896]{2,1,0:T(1,128)}), s32[8,1,896]{2,1,0:T(1,128)S(1)}, u32[]{:S(2)}, u32[]{:S(2)}) %all-to-all-start.1) | async-done | bytes 28704 | tf_op jit(solution)/shard_map/all_to_all | solution.py:12
  87.7 0.5 broadcast.10
  88.2 0.7 reduce.1
  88.9 0.1 reshape.27
  89.0 0.1 copy.26
  89.1 0.1 shift_right_arithmetic.23
  89.1 0.3 copy.27
  89.5 33.7 %reduce-scatter.3.cloned.1.call-done = bf16[128,3584]{1,0:T(8,128)(2,1)} async-done(((bf16[512,3584]{1,0:T(8,128)(2,1)}), bf16[128,3584]{1,0:T(8,128)(2,1)}) %reduce-scatter.3.cloned.1.call-update) | async-done | bytes 917520 | tf_op jit(solution)/shard_map/reduce_scatter | solution.py:31
  123.1 1.4 convert_element_type.42
  124.5 1.1 fusion.1
  125.6 0.0 all-gather.5.cloned.1.call-update
  125.6 0.0 reduce-scatter.5.cloned.1.call-start
  125.7 33.1 %all-gather.5.cloned.1.call-done = bf16[512,1792]{1,0:T(8,128)(2,1)} async-done(((bf16[128,1792]{1,0:T(8,128)(2,1)}), bf16[512,1792]{1,0:T(8,128)(2,1)}) %all-gather.5.cloned.1.call-update) | async-done | bytes 1835024 | tf_op jit(solution)/shard_map/all_gather | solution.py:41
  158.8 8.9 %convolution_convert_fusion = bf16[512,2048]{1,0:T(8,128)(2,1)} fusion(bf16[512,1792]{1,0:T(8,128)(2,1)} %all-gather.5.cloned.1.call-done, bf16[1792,2048]{1,0:T(8,128)(2,1)} %param.11), kind=kOutput, calls=%fused_computation.3 | convolution fusion | flops 3759144960 | bytes 11272192 | tf_op jit(solution)/shard_map/dot_general | solution.py:40
  167.7 0.0 reduce-scatter.5.cloned.1.call-update
  167.7 36.2 %reduce-scatter.5.cloned.1.call-done = bf16[64,2048]{1,0:T(8,128)(2,1)} async-done(((bf16[512,2048]{1,0:T(8,128)(2,1)}), bf16[64,2048]{1,0:T(8,128)(2,1)}) %reduce-scatter.5.cloned.1.call-update) | async-done | bytes 262160 | tf_op jit(solution)/shard_map/reduce_scatter | solution.py:45
  204.0 1.9 multiply_reduce_fusion.1
  205.9 9.8 %psum.15 = f32[64]{0:T(128)S(1)} all-reduce(f32[64]{0:T(128)S(1)} %get-tuple-element.2), channel_id=1, replica_groups=mesh['dp'=4,'tensor'=8] {'dp'}, use_global_device_ids=true, to_apply=%region_5.6 | all-reduce | flops 64 | bytes 512 | tf_op jit(solution)/shard_map/psum | solution.py:53
  215.7 0.5 broadcast_multiply_fusion
  (4 shorter events, 0.0 us)
Async XLA Ops:
  7.2 40.9 %all-gather.3.cloned.1.call-start = ((), (), s32[]{:S(2)}) async-start(), calls=%async_computation.4 | async-start | bytes 2359296 | tf_op jit(solution)/shard_map/all_gather | solution.py:19
  19.0 104.1 %reduce-scatter.3.cloned.1.call-start = ((), (), s32[]{:S(2)}) async-start(), calls=%async_computation.5 | async-start | bytes 4587520 | tf_op jit(solution)/shard_map/reduce_scatter | solution.py:31
  48.1 2.2 copy-start
  50.3 17.5 %copy-start.1 = (bf16[4,8,16,2048]{3,2,1,0:T(8,128)(2,1)}, bf16[4,8,16,2048]{3,2,1,0:T(8,128)(2,1)S(1)}, u32[]{:S(2)}) copy-start(bf16[4,8,16,2048]{3,2,1,0:T(8,128)(2,1)S(1)} %copy.23) | copy-start | bytes 6291460
  77.1 0.8 copy-start.2
  78.7 9.0 %all-to-all-start.1 = ((s32[8,1,896]{2,1,0:T(1,128)}), s32[8,1,896]{2,1,0:T(1,128)S(1)}, u32[]{:S(2)}, u32[]{:S(2)}) async-start(s32[8,1,896]{2,1,0:T(1,128)} %reshape.26), calls=%async_computation.2 | async-start | bytes 57344 | tf_op jit(solution)/shard_map/all_to_all | solution.py:12
  82.0 76.8 %all-gather.5.cloned.1.call-start = ((), (), s32[]{:S(2)}) async-start(), calls=%async_computation.6 | async-start | bytes 2293760 | tf_op jit(solution)/shard_map/all_gather | solution.py:41
  125.6 78.3 %reduce-scatter.5.cloned.1.call-start = ((), (), s32[]{:S(2)}) async-start(), calls=%async_computation.7 | async-start | bytes 2359296 | tf_op jit(solution)/shard_map/reduce_scatter | solution.py:45
Sparse Core Ops, SparseCore 0:
  19.1 28.8 all-gather.2
  77.2 45.8 reduce-scatter.2
  125.7 33.0 all-gather.4
  167.8 36.0 reduce-scatter.4
where the time goes:
time: 223 us
  waiting for transfers between devices  137 us (61%)
  blocking collectives  30.4 us (14%)
  matrix products  23.1 us (10%)
  between operations  13.9 us (6%)
  other arithmetic  8.92 us (4%)
  local copies, waits for them, and re-layouts  5.94 us (3%)
  starting transfers between devices  3.51 us (2%)
    reduce_scatter x1, waiting for transfers between devices, on_device(): lax.psum_scatter(partial_value.astype(jnp.bfloat16), 'tensor', scatter_di...  36.2 us
    reduce_scatter x1, waiting for transfers between devices, on_device(): lax.psum_scatter(jnp.concatenate((gate_part, up_part), axis=1).astype(jnp...  33.7 us
    all_gather x1, waiting for transfers between devices, on_device(): lax.all_gather(hidden, 'dp', axis=0, tiled=True)  33.1 us
    all_gather x1, waiting for transfers between devices, on_device(): collected = lax.all_gather(columns, 'tensor', axis=0, tiled=True)  28.3 us
    all_to_all x1, blocking collectives, on_device(): lax.all_to_all(saved_input, 'dp', split_axis=1, concat_axis=0, tiled=True)  10.8 us
    psum x1, blocking collectives, on_device(): squares = lax.psum(jnp.sum(widened * widened, axis=1), 'dp')  9.83 us
    psum x1, blocking collectives, on_device(): row_check = lax.psum(jnp.sum(widened_out * widened_out, axis=1), 'dp') / D  9.79 us
    dot_general x1, matrix products, on_device(): jnp.dot(lax.all_gather(hidden, 'dp', axis=0, tiled=True), down_weight, pr...  8.89 us
  transfers between devices with their start and end apart: 5, of which 5 were waited for; matrix products, arithmetic and copies ran while one was open for 1% of the time, Pallas kernels for 0%

commit v1 on v0

--- a/solution.py
+++ b/solution.py
@@ -1,6 +1,8 @@
 import jax
 import jax.numpy as jnp
 from jax import lax
+from jax.experimental import pallas as pl
+from jax.experimental.pallas import tpu as pltpu
 from jax.sharding import PartitionSpec as P
 
 D = 8192
@@ -54,6 +56,322 @@
     return (layer_out, row_check)
 
 
+MESH = pl.DeviceIdType.MESH
+F32 = jnp.float32
+BF16 = jnp.bfloat16
+
+
+def fused(
+    x_ref, kb_ref, gain_ref, wg_hbm, wu_hbm, wd_hbm, out_ref, chk_ref,
+    wg, wu, wd, xbuf, xn, kw, kall, iown, iall, keep,
+    pd, py, px, pown, relay, from_x, from_y, hbuf, qf, qb, sib, ssend, acc, zr, cown, call,
+    w_sem, rx, tx_dp, tx_z, tx_s, rk, tk, ri, ti, rp, tp, rh, th, rs, ts, rz, tz, rc, tc,
+):
+    m, R = xbuf.shape[1], xbuf.shape[2]
+    width = xbuf.shape[3]
+    TB = m * R
+    U = wg.shape[1]
+    half_rows = out_ref.shape[0]
+    words = kb_ref.shape[1] // m
+    chips = m // 2
+    tile = 256 if U % 256 == 0 and width % 256 == 0 else 128
+    cut = (U // tile + 1) // 2 * tile
+    parts = ((0, cut), (cut, U - cut))
+
+    i, j = lax.axis_index("dp"), lax.axis_index("tensor")
+    iy, ix = i // 2, i % 2
+    z, c = j // 2, j % 2
+    xnb = iy * 2 + (1 - ix)
+    ynb = (1 - iy) * 2 + ix
+    diag = (1 - iy) * 2 + (1 - ix)
+    sibling = z * 2 + (1 - c)
+    sends = []
+
+    def send(src, dst, ss, rsem, to):
+        copy = pltpu.make_async_remote_copy(
+            src_ref=src, dst_ref=dst, send_sem=ss, recv_sem=rsem, device_id=to, device_id_type=MESH
+        )
+        copy.start()
+        sends.append(copy)
+
+    def arrived(dst, rsem):
+        pltpu.make_async_remote_copy(
+            src_ref=dst, dst_ref=dst, send_sem=tc.at[0], recv_sem=rsem,
+            device_id=(i, sibling), device_id_type=MESH,
+        ).wait_recv()
+
+    loads = [pltpu.make_async_copy(s, d, w_sem.at[k]) for k, (s, d) in enumerate(((wg_hbm, wg), (wu_hbm, wu), (wd_hbm, wd)))]
+    for load in loads:
+        load.start()
+
+    barrier = pltpu.get_barrier_semaphore()
+    for other in (xnb, ynb, diag):
+        pl.semaphore_signal(barrier, inc=1, device_id=(other, j), device_id_type=MESH)
+    for step in range(1, m):
+        pl.semaphore_signal(barrier, inc=1, device_id=(i, (j + step) % m), device_id_type=MESH)
+    xbuf[i, j] = x_ref[:, pl.ds(pl.multiple_of(i * width, width), width)]
+    pl.semaphore_wait(barrier, 3 + m - 1)
+
+    for k, other in enumerate((diag, ynb, xnb)):
+        send(x_ref.at[:, pl.ds(pl.multiple_of(other * width, width), width)], xbuf.at[i, j], tx_dp.at[k], rx.at[i, j], (other, j))
+
+    kw[...] = jnp.zeros_like(kw)
+    for t in range(m):
+        kw[t, :, 0:words] = kb_ref[:, t * words : (t + 1) * words]
+    rows = x_ref[...].astype(F32)
+    total = jnp.sum(rows * rows, axis=1, keepdims=True)
+    iown[...] = jnp.broadcast_to(lax.rsqrt(total / (x_ref.shape[1]) + 1e-05), iown.shape)
+    iall[j] = iown[...]
+    kall[j] = kw[j]
+
+    order = (diag, ynb, xnb, i)
+    for k, b in enumerate(order):
+        if k < 3:
+            arrived(xbuf.at[b, j], rx.at[b, j])
+        for step in range(1, chips):
+            to = ((z + step) % chips) * 2 + c
+            send(xbuf.at[b, j], xbuf.at[b, j], tx_z.at[k, step - 1], rx.at[b, j], (i, to))
+        send(xbuf.at[b, j], xbuf.at[b, j], tx_s.at[k, 0], rx.at[b, j], (i, sibling))
+    for step in range(1, m):
+        to = (j + step) % m
+        send(kw.at[to], kall.at[j], tk.at[step - 1], rk.at[j], (i, to))
+        send(iown, iall.at[j], ti.at[step - 1], ri.at[j], (i, to))
+
+    gain = gain_ref[...].astype(F32)
+
+    def collect(k):
+        b = order[k]
+        for step in range(1, chips):
+            slot = ((z + step) % chips) * 2 + c
+            arrived(xbuf.at[b, slot], rx.at[b, slot])
+            send(xbuf.at[b, slot], xbuf.at[b, slot], tx_s.at[k, step], rx.at[b, slot], (i, sibling))
+        for step in range(chips):
+            slot = ((z + step) % chips) * 2 + (1 - c)
+            arrived(xbuf.at[b, slot], rx.at[b, slot])
+
+        def scale(t, carry):
+            xn[k, pl.ds(pl.multiple_of(t * R, R), R), :] = (xbuf[b, t].astype(F32) * gain).astype(BF16)
+            return carry
+
+        lax.fori_loop(0, m, scale, 0)
+
+    def project(k, w, dst, lo=0, hi=U, extra=None):
+        def body(t, carry):
+            cols = pl.ds(pl.multiple_of(t * tile, tile), tile)
+            part = jnp.dot(xn[k], w[:, cols], preferred_element_type=F32)
+            if extra is not None:
+                part = part + extra[:, cols].astype(F32)
+            dst[:, cols] = part.astype(dst.dtype)
+            return carry
+
+        lax.fori_loop(lo // tile, hi // tile, body, 0)
+
+    collect(0)
+    loads[0].wait()
+    loads[1].wait()
+    for p, (lo, size) in enumerate(parts):
+        cols = pl.ds(lo, size)
+        project(0, wg, pd.at[0], lo, lo + size)
+        send(pd.at[0, :, cols], relay.at[0, :, cols], tp.at[p, 0], rp.at[p, 0], (xnb, j))
+        project(0, wu, pd.at[1], lo, lo + size)
+        send(pd.at[1, :, cols], relay.at[1, :, cols], tp.at[p, 1], rp.at[p, 1], (ynb, j))
+        if p == 0:
+            collect(1)
+        project(1, wu, py.at[1], lo, lo + size)
+        send(py.at[1, :, cols], from_y.at[1, :, cols], tp.at[p, 2], rp.at[p, 2], (ynb, j))
+        if p == 0:
+            collect(2)
+        project(2, wg, px.at[0], lo, lo + size)
+        send(px.at[0, :, cols], from_x.at[0, :, cols], tp.at[p, 3], rp.at[p, 3], (xnb, j))
+        if p == 0:
+            collect(3)
+    for p, (lo, size) in enumerate(parts):
+        cols = pl.ds(lo, size)
+        arrived(relay.at[0, :, cols], rp.at[p, 0])
+        project(1, wg, py.at[0], lo, lo + size, relay.at[0])
+        send(py.at[0, :, cols], from_y.at[0, :, cols], tp.at[p, 4], rp.at[p, 4], (ynb, j))
+        arrived(relay.at[1, :, cols], rp.at[p, 1])
+        project(2, wu, px.at[1], lo, lo + size, relay.at[1])
+        send(px.at[1, :, cols], from_x.at[1, :, cols], tp.at[p, 5], rp.at[p, 5], (xnb, j))
+    project(3, wg, pown.at[0])
+    project(3, wu, pown.at[1])
+
+    for step in range(1, m):
+        slot = (j + step) % m
+        arrived(kall.at[slot], rk.at[slot])
+        arrived(iall.at[slot], ri.at[slot])
+    word = kall[...].reshape(TB, kall.shape[2])
+    scale_rows = iall[...].reshape(TB, iall.shape[2])[:, 0:1]
+    byte = [jnp.bitwise_and(jnp.right_shift(word, 8 * q), 255).astype(F32).astype(BF16) for q in range(4)]
+    lanes = kall.shape[2]
+
+    def expand(t, carry):
+        unit = t * tile + lax.broadcasted_iota(jnp.int32, (lanes, tile), 1)
+        where = lax.broadcasted_iota(jnp.int32, (lanes, tile), 0)
+        spread = jnp.zeros((TB, tile), F32)
+        for q in range(4):
+            hit = (jnp.right_shift(unit, 3) == where * 4 + q)
+            spread += jnp.dot(byte[q], jnp.where(hit, 1.0, 0.0).astype(BF16), preferred_element_type=F32)
+        shift = jnp.bitwise_and(lax.broadcasted_iota(jnp.int32, (TB, tile), 1), 7)
+        bit = jnp.bitwise_and(jnp.right_shift(spread.astype(jnp.int32), shift), 1)
+        keep[:, pl.ds(pl.multiple_of(t * tile, tile), tile)] = (2 * bit).astype(F32)
+        return carry
+
+    lax.fori_loop(0, U // tile, expand, 0)
+
+    for p, (lo, size) in enumerate(parts):
+        cols = pl.ds(lo, size)
+        arrived(from_y.at[1, :, cols], rp.at[p, 2])
+        arrived(from_x.at[0, :, cols], rp.at[p, 3])
+        arrived(from_y.at[0, :, cols], rp.at[p, 4])
+        arrived(from_x.at[1, :, cols], rp.at[p, 5])
+
+        def activate(t, carry):
+            at = pl.ds(pl.multiple_of(t * tile, tile), tile)
+            gate = (pown[0, :, at] + from_x[0, :, at].astype(F32) + from_y[0, :, at].astype(F32)) * scale_rows
+            up = (pown[1, :, at] + from_x[1, :, at].astype(F32) + from_y[1, :, at].astype(F32)) * scale_rows
+            hbuf[i, :, at] = (gate / (1.0 + jnp.exp(-gate)) * up * keep[:, at]).astype(BF16)
+            return carry
+
+        lax.fori_loop(lo // tile, (lo + size) // tile, activate, 0)
+        send(hbuf.at[i, :, cols], hbuf.at[i, :, cols], th.at[p, 0], rh.at[i, p], (xnb, j))
+        send(hbuf.at[i, :, cols], hbuf.at[i, :, cols], th.at[p, 1], rh.at[i, p], (ynb, j))
+
+    loads[2].wait()
+    blocks = (i, xnb, ynb, diag)
+
+    def down(k):
+        b = blocks[k]
+
+        def body(t, carry):
+            cols = pl.ds(pl.multiple_of(t * tile, tile), tile)
+            part = jnp.dot(hbuf[b], wd[:, cols], preferred_element_type=F32)
+            for h in range(2):
+                piece = part[h * half_rows : (h + 1) * half_rows]
+                qf[k, h, :, cols] = piece
+                qb[k, h, :, cols] = piece.astype(BF16)
+            return carry
+
+        lax.fori_loop(0, width // tile, body, 0)
+        send(qb.at[k, 1 - c], sib.at[k], ts.at[k], rs.at[k], (i, sibling))
+
+    z_sends = []
+
+    def pair(k):
+        b = blocks[k]
+        arrived(sib.at[k], rs.at[k])
+        both = qf[k, c] + sib[k].astype(F32)
+        copy = pltpu.make_async_remote_copy(
+            src_ref=ssend.at[k], dst_ref=zr.at[z], send_sem=tz.at[k], recv_sem=rz.at[z],
+            device_id=(i, b * 2 + c), device_id_type=MESH,
+        )
+
+        @pl.when(b == z)
+        def _():
+            acc[...] = both
+
+        @pl.when(b != z)
+        def _():
+            ssend[k] = both.astype(BF16)
+            copy.start()
+
+        z_sends.append((b, copy))
+
+    down(0)
+    p0, p1 = (pl.ds(lo, size) for lo, size in parts)
+    arrived(hbuf.at[xnb, :, p0], rh.at[xnb, 0])
+    send(hbuf.at[xnb, :, p0], hbuf.at[xnb, :, p0], th.at[0, 2], rh.at[xnb, 0], (ynb, j))
+    pair(0)
+    arrived(hbuf.at[ynb, :, p0], rh.at[ynb, 0])
+    arrived(hbuf.at[ynb, :, p1], rh.at[ynb, 1])
+    send(hbuf.at[ynb, :, p1], hbuf.at[ynb, :, p1], th.at[1, 2], rh.at[ynb, 1], (xnb, j))
+    arrived(hbuf.at[xnb, :, p1], rh.at[xnb, 1])
+    down(1)
+    down(2)
+    pair(1)
+    pair(2)
+    arrived(hbuf.at[diag, :, p0], rh.at[diag, 0])
+    arrived(hbuf.at[diag, :, p1], rh.at[diag, 1])
+    down(3)
+    pair(3)
+
+    first = j * (half_rows // R)
+    mine = xbuf.reshape(xbuf.shape[0] * m, R, width)
+    value = acc[...]
+    for step in range(1, chips):
+        slot = (z + step) % chips
+        arrived(zr.at[slot], rz.at[slot])
+        value = value + zr[slot].astype(F32)
+    acc[...] = value
+    sums = []
+    for q in range(half_rows // R):
+        rows_q = pl.ds(q * R, R)
+        result = (mine[first + q].astype(F32) + acc[rows_q, :]).astype(BF16)
+        out_ref[rows_q, :] = result
+        wide = result.astype(F32)
+        cown[rows_q, :] = jnp.broadcast_to(jnp.sum(wide * wide, axis=1, keepdims=True), (R, cown.shape[1]))
+    for k, other in enumerate((xnb, ynb, diag)):
+        send(cown, call.at[i], tc.at[k], rc.at[i], (other, j))
+    check = cown[...]
+    for other in (xnb, ynb, diag):
+        arrived(call.at[other], rc.at[other])
+        check = check + call[other]
+    chk_ref[...] = check / x_ref.shape[1]
+
+    for copy in sends:
+        copy.wait_send()
+    for b, copy in z_sends:
+
+        @pl.when(b != z)
+        def _():
+            copy.wait_send()
+
+
+def on_plane(saved_input, keep_bits, norm_gain, gate_weight, up_weight, down_weight):
+    n, m = lax.axis_size("dp"), lax.axis_size("tensor")
+    R, full = saved_input.shape
+    width, U = gate_weight.shape
+    TB = R * m
+    out_rows = n * TB // m
+    chips = m // 2
+    lanes = -(-(keep_bits.shape[1] // m) // 128) * 128
+    dma = pltpu.SemaphoreType.DMA
+    vmem = pl.BlockSpec(memory_space=pltpu.VMEM)
+    hbm = pl.BlockSpec(memory_space=pl.ANY)
+    scratch = [
+        pltpu.VMEM((width, U), BF16), pltpu.VMEM((width, U), BF16), pltpu.VMEM((U, width), BF16),
+        pltpu.VMEM((n, m, R, width), BF16), pltpu.VMEM((n, TB, width), BF16),
+        pltpu.VMEM((m, R, lanes), jnp.int32), pltpu.VMEM((m, R, lanes), jnp.int32),
+        pltpu.VMEM((R, 128), F32), pltpu.VMEM((m, R, 128), F32), pltpu.VMEM((TB, U), F32),
+        pltpu.VMEM((2, TB, U), BF16), pltpu.VMEM((2, TB, U), BF16), pltpu.VMEM((2, TB, U), BF16),
+        pltpu.VMEM((2, TB, U), F32), pltpu.VMEM((2, TB, U), BF16),
+        pltpu.VMEM((2, TB, U), BF16), pltpu.VMEM((2, TB, U), BF16),
+        pltpu.VMEM((n, TB, U), BF16),
+        pltpu.VMEM((n, 2, out_rows, width), F32), pltpu.VMEM((n, 2, out_rows, width), BF16),
+        pltpu.VMEM((n, out_rows, width), BF16), pltpu.VMEM((n, out_rows, width), BF16),
+        pltpu.VMEM((out_rows, width), F32), pltpu.VMEM((chips, out_rows, width), BF16),
+        pltpu.VMEM((out_rows, 128), F32), pltpu.VMEM((n, out_rows, 128), F32),
+        dma((3,)), dma((n, m)), dma((3,)), dma((n, chips - 1)), dma((n, chips)),
+        dma((m,)), dma((m - 1,)), dma((m,)), dma((m - 1,)),
+        dma((2, 6)), dma((2, 6)), dma((n, 2)), dma((2, 3)),
+        dma((n,)), dma((n,)), dma((chips,)), dma((n,)), dma((n,)), dma((3,)),
+    ]
+    layer_out, check = pl.pallas_call(
+        fused,
+        out_shape=(
+            jax.ShapeDtypeStruct((out_rows, width), BF16),
+            jax.ShapeDtypeStruct((out_rows, 128), F32),
+        ),
+        in_specs=[vmem, vmem, vmem, hbm, hbm, hbm],
+        out_specs=(vmem, vmem),
+        scratch_shapes=scratch,
+        compiler_params=pltpu.CompilerParams(
+            collective_id=0, has_side_effects=True, vmem_limit_bytes=60 * 1024 * 1024
+        ),
+    )(saved_input, keep_bits, norm_gain.reshape(1, width), gate_weight, up_weight, down_weight)
+    return layer_out, check[:, 0]
+
+
 def solution(mesh):
     placed = (
         P(("dp", "tensor"), None),
@@ -63,8 +381,9 @@
         P("dp", "tensor"),
         P("tensor", "dp"),
     )
+    plane = mesh.shape["dp"] == 4 and mesh.shape["tensor"] == 2 * mesh.shape["dp"]
     return jax.shard_map(
-        on_device,
+        on_plane if plane else on_device,
         mesh=mesh,
         in_specs=placed,
         out_specs=(P("tensor", "dp"), P("tensor")),

time: 223 us -> 113 us (0.51)
  waiting for transfers between devices: 137 us -> 0 us
  Pallas kernels: 0 us -> 107 us
  blocking collectives: 30.4 us -> 0 us
  matrix products: 23.1 us -> 0 us
  between operations: 13.9 us -> 0.64 us
  other arithmetic: 8.92 us -> 0 us
  starting transfers between devices: 3.51 us -> 0 us
    pallas_call x0 -> x1, Pallas kernels: none -> 107 us  [on_plane(): pl.pallas_call(fused, out_shape=(jax.ShapeDtypeStruct((out_rows, width),...]
    reduce_scatter x2 -> x0, waiting for transfers between devices: 69.9 us -> none  [the longest x1 36.2 us: on_device(): lax.psum_scatter(partial_value.astype(jnp.bfloat16), 'tensor', scatter_di...]
    all_gather x2 -> x0, waiting for transfers between devices: 61.4 us -> none  [the longest x1 33.1 us: on_device(): lax.all_gather(hidden, 'dp', axis=0, tiled=True)]
    dot_general x3 -> x0, matrix products: 23.1 us -> none  [the longest x1 8.89 us: on_device(): jnp.dot(lax.all_gather(hidden, 'dp', axis=0, tiled=True), down_weight, pr...]
    psum x2 -> x0, blocking collectives: 19.6 us -> none  [the longest x1 9.83 us: on_device(): squares = lax.psum(jnp.sum(widened * widened, axis=1), 'dp')]
    all_to_all x1 -> x0, blocking collectives: 10.8 us -> none  [on_device(): lax.all_to_all(saved_input, 'dp', split_axis=1, concat_axis=0, tiled=True)]
    all_to_all x1 -> x0, waiting for transfers between devices: 5.52 us -> none  [on_device(): lax.all_to_all(keep_bits, 'tensor', split_axis=1, concat_axis=0, tiled=True)]
    all_to_all x1 -> x0, starting transfers between devices: 3.35 us -> none  [on_device(): lax.all_to_all(keep_bits, 'tensor', split_axis=1, concat_axis=0, tiled=True)]
  transfers between devices with their start and end apart: 5 -> 0, of which waited for: 5 -> 0; matrix products, arithmetic and copies ran while one was open for 1% -> 0% of each run, Pallas kernels for 0% -> 0%
where the time goes in v1:
time: 113 us; the launch traced here: 112 us
  Pallas kernels  107 us (95%)
  local copies, waits for them, and re-layouts  4.34 us (4%)
    pallas_call x1, Pallas kernels, on_plane(): pl.pallas_call(fused, out_shape=(jax.ShapeDtypeStruct((out_rows, width),...  107 us

profile of v1, /device:TPU:0, one launch (start us, length us, event | category | flops | bytes accessed | tf_op | source)
XLA Modules:
  0.0 112.4 jit_solution(3196991043917103548)
XLA Ops:
  0.6 1.3 %reshape.7.gain_ref = bf16[1,2048]{1,0:T(2,128)(2,1)} reshape(bf16[2048]{0:T(1024)(128)(2,1)} %param.8) | data formatting | bytes 8192 | tf_op jit(solution)/shard_map/reshape | solution.py:371
  1.9 107.4 %shard_map.77 = (bf16[64,2048]{1,0:T(8,128)(2,1)}, f32[64,128]{1,0:T(8,128)}) custom-call(bf16[16,8192]{1,0:T(8,128)(2,1)} %x_ref.1, s32[16,448]{1,0:T(8,128)} %kb_ref.1, bf16[1,2048]{1,0:T(2,128)(2,1)} %reshape.7.gain_ref, bf16[2048,1792]{1,0:T(8,128)(2,1)} %wg_hbm.1, bf16[2048,1792]{1,0:T(8,128)(2,1)} %wu_hbm.1, bf16[1792,2048]{1,0:T(8,128)(2,1)} %wd_hbm.1), custom_call_target="tpu_custom_call" | custom-call | tf_op jit(solution)/shard_map/pallas_call | solution.py:359
  109.4 1.4 %slice_reduce_fusion = f32[64]{0:T(128)} fusion(f32[64,128]{1,0:T(8,128)} %get-tuple-element.5), kind=kLoop, calls=%fused_computation | loop fusion | bytes 512 | tf_op jit(solution)/shard_map/slice | solution.py:372
  110.7 1.7 %copy.9 = bf16[64,2048]{1,0:T(8,128)(2,1)} copy(bf16[64,2048]{1,0:T(8,128)(2,1)} %get-tuple-element.8) | data formatting | bytes 524288

commit v2 on v1

--- a/solution.py
+++ b/solution.py
@@ -59,13 +59,14 @@
 MESH = pl.DeviceIdType.MESH
 F32 = jnp.float32
 BF16 = jnp.bfloat16
+COL_PARTS = 4
 
 
 def fused(
     x_ref, kb_ref, gain_ref, wg_hbm, wu_hbm, wd_hbm, out_ref, chk_ref,
     wg, wu, wd, xbuf, xn, kw, kall, iown, iall, keep,
-    pd, py, px, pown, relay, from_x, from_y, hbuf, qf, qb, sib, ssend, acc, zr, cown, call,
-    w_sem, rx, tx_dp, tx_z, tx_s, rk, tk, ri, ti, rp, tp, rh, th, rs, ts, rz, tz, rc, tc,
+    pd, py, px, pown, relay, from_x, from_y, hbuf, qf, qb, sib, ssend, acc, zr, zpass, cown, call,
+    w_sem, rx, tx_dp, tx_z, tx_s, rk, tk, ri, ti, rp, tp, rh, th, rs, ts, rz, rpass, tz, rc, tc,
 ):
     m, R = xbuf.shape[1], xbuf.shape[2]
     width = xbuf.shape[3]
@@ -73,10 +74,9 @@
     U = wg.shape[1]
     half_rows = out_ref.shape[0]
     words = kb_ref.shape[1] // m
-    chips = m // 2
     tile = 256 if U % 256 == 0 and width % 256 == 0 else 128
-    cut = (U // tile + 1) // 2 * tile
-    parts = ((0, cut), (cut, U - cut))
+    step_cols = -(-(U // tile) // COL_PARTS) * tile
+    parts = tuple((lo, min(step_cols, U - lo)) for lo in range(0, U, step_cols))
 
     i, j = lax.axis_index("dp"), lax.axis_index("tensor")
     iy, ix = i // 2, i % 2
@@ -85,7 +85,10 @@
     ynb = (1 - iy) * 2 + ix
     diag = (1 - iy) * 2 + (1 - ix)
     sibling = z * 2 + (1 - c)
-    sends = []
+    mate = z + 1 - 2 * (z % 2)
+    far, far_end = 2 - z // 2, 3 * (1 - z // 2)
+    inner = (z + 1) // 2 == 1
+    sends, inner_sends = [], []
 
     def send(src, dst, ss, rsem, to):
         copy = pltpu.make_async_remote_copy(
@@ -128,25 +131,30 @@
     for k, b in enumerate(order):
         if k < 3:
             arrived(xbuf.at[b, j], rx.at[b, j])
-        for step in range(1, chips):
-            to = ((z + step) % chips) * 2 + c
-            send(xbuf.at[b, j], xbuf.at[b, j], tx_z.at[k, step - 1], rx.at[b, j], (i, to))
+        for q, to in enumerate((mate, far)):
+            send(xbuf.at[b, j], xbuf.at[b, j], tx_z.at[k, q], rx.at[b, j], (i, to * 2 + c))
         send(xbuf.at[b, j], xbuf.at[b, j], tx_s.at[k, 0], rx.at[b, j], (i, sibling))
-    for step in range(1, m):
-        to = (j + step) % m
-        send(kw.at[to], kall.at[j], tk.at[step - 1], rk.at[j], (i, to))
-        send(iown, iall.at[j], ti.at[step - 1], ri.at[j], (i, to))
-
-    gain = gain_ref[...].astype(F32)
+
+    gain = gain_ref[...].astype(F32).reshape(1, width)
+
+    def forward(k):
+        b = order[k]
+        for q, chip in enumerate((mate, far, far_end)):
+            slot = chip * 2 + c
+            arrived(xbuf.at[b, slot], rx.at[b, slot])
+            if q > 0:
+                copy = pltpu.make_async_remote_copy(
+                    src_ref=xbuf.at[b, slot], dst_ref=xbuf.at[b, slot], send_sem=tx_z.at[k, q + 1],
+                    recv_sem=rx.at[b, slot], device_id=(i, mate * 2 + c), device_id_type=MESH,
+                )
+                pl.when(inner)(copy.start)
+                inner_sends.append(copy)
+            send(xbuf.at[b, slot], xbuf.at[b, slot], tx_s.at[k, q + 1], rx.at[b, slot], (i, sibling))
 
     def collect(k):
         b = order[k]
-        for step in range(1, chips):
-            slot = ((z + step) % chips) * 2 + c
-            arrived(xbuf.at[b, slot], rx.at[b, slot])
-            send(xbuf.at[b, slot], xbuf.at[b, slot], tx_s.at[k, step], rx.at[b, slot], (i, sibling))
-        for step in range(chips):
-            slot = ((z + step) % chips) * 2 + (1 - c)
+        for chip in (z, mate, far, far_end):
+            slot = chip * 2 + (1 - c)
             arrived(xbuf.at[b, slot], rx.at[b, slot])
 
         def scale(t, carry):
@@ -166,6 +174,13 @@
 
         lax.fori_loop(lo // tile, hi // tile, body, 0)
 
+    def stage(k, w, dst, to, land, slot):
+        for p, (lo, size) in enumerate(parts):
+            cols = pl.ds(lo, size)
+            project(k, w, dst, lo, lo + size)
+            send(dst.at[:, cols], land.at[:, cols], tp.at[p, slot], rp.at[p, slot], (to, j))
+
+    forward(0)
     collect(0)
     loads[0].wait()
     loads[1].wait()
@@ -175,16 +190,13 @@
         send(pd.at[0, :, cols], relay.at[0, :, cols], tp.at[p, 0], rp.at[p, 0], (xnb, j))
         project(0, wu, pd.at[1], lo, lo + size)
         send(pd.at[1, :, cols], relay.at[1, :, cols], tp.at[p, 1], rp.at[p, 1], (ynb, j))
-        if p == 0:
-            collect(1)
-        project(1, wu, py.at[1], lo, lo + size)
-        send(py.at[1, :, cols], from_y.at[1, :, cols], tp.at[p, 2], rp.at[p, 2], (ynb, j))
-        if p == 0:
-            collect(2)
-        project(2, wg, px.at[0], lo, lo + size)
-        send(px.at[0, :, cols], from_x.at[0, :, cols], tp.at[p, 3], rp.at[p, 3], (xnb, j))
-        if p == 0:
-            collect(3)
+    forward(1)
+    collect(1)
+    stage(1, wu, py.at[1], ynb, from_y.at[1], 2)
+    forward(2)
+    collect(2)
+    stage(2, wg, px.at[0], xnb, from_x.at[0], 3)
+    forward(3)
     for p, (lo, size) in enumerate(parts):
         cols = pl.ds(lo, size)
         arrived(relay.at[0, :, cols], rp.at[p, 0])
@@ -193,6 +205,11 @@
         arrived(relay.at[1, :, cols], rp.at[p, 1])
         project(2, wu, px.at[1], lo, lo + size, relay.at[1])
         send(px.at[1, :, cols], from_x.at[1, :, cols], tp.at[p, 5], rp.at[p, 5], (xnb, j))
+    for step in range(1, m):
+        to = (j + step) % m
+        send(kw.at[to], kall.at[j], tk.at[step - 1], rk.at[j], (i, to))
+        send(iown, iall.at[j], ti.at[step - 1], ri.at[j], (i, to))
+    collect(3)
     project(3, wg, pown.at[0])
     project(3, wu, pown.at[1])
 
@@ -240,67 +257,120 @@
     loads[2].wait()
     blocks = (i, xnb, ynb, diag)
 
-    def down(k):
+    span = width // 2
+    halves = [pl.ds(h * span, span) for h in range(2)]
+
+    def down(k, h):
         b = blocks[k]
 
         def body(t, carry):
             cols = pl.ds(pl.multiple_of(t * tile, tile), tile)
             part = jnp.dot(hbuf[b], wd[:, cols], preferred_element_type=F32)
-            for h in range(2):
-                piece = part[h * half_rows : (h + 1) * half_rows]
-                qf[k, h, :, cols] = piece
-                qb[k, h, :, cols] = piece.astype(BF16)
+            for r in range(2):
+                piece = part[r * half_rows : (r + 1) * half_rows]
+                qf[k, r, :, cols] = piece
+                qb[k, r, :, cols] = piece.astype(BF16)
             return carry
 
-        lax.fori_loop(0, width // tile, body, 0)
-        send(qb.at[k, 1 - c], sib.at[k], ts.at[k], rs.at[k], (i, sibling))
-
-    z_sends = []
-
-    def pair(k):
-        b = blocks[k]
-        arrived(sib.at[k], rs.at[k])
-        both = qf[k, c] + sib[k].astype(F32)
-        copy = pltpu.make_async_remote_copy(
-            src_ref=ssend.at[k], dst_ref=zr.at[z], send_sem=tz.at[k], recv_sem=rz.at[z],
-            device_id=(i, b * 2 + c), device_id_type=MESH,
-        )
-
-        @pl.when(b == z)
+        lax.fori_loop(h * span // tile, (h + 1) * span // tile, body, 0)
+        at = halves[h]
+        send(qb.at[k, 1 - c, :, at], sib.at[k, :, at], ts.at[k, h], rs.at[k, h], (i, sibling))
+
+    away_sends = []
+
+    def pair(k, h):
+        b, at = blocks[k], halves[h]
+        arrived(sib.at[k, :, at], rs.at[k, h])
+        qf[k, c, :, at] = qf[k, c, :, at] + sib[k, :, at].astype(F32)
+        here, near = b == z, b == mate
+        away = b // 2 != z // 2
+        outer = (z + 1) // 2 != 1
+
+        def copy_to(dst, rsem, chip):
+            return pltpu.make_async_remote_copy(
+                src_ref=ssend.at[k, :, at], dst_ref=dst, send_sem=tz.at[k, h], recv_sem=rsem,
+                device_id=(i, chip * 2 + c), device_id_type=MESH,
+            )
+
+        direct = copy_to(zr.at[0, :, at], rz.at[0, h], mate)
+        passed = copy_to(zpass.at[b, :, at], rpass.at[b, h], mate)
+        joined = copy_to(zr.at[1, :, at], rz.at[1, h], b)
+
+        @pl.when(here)
         def _():
-            acc[...] = both
-
-        @pl.when(b != z)
+            acc[:, at] = qf[k, c, :, at]
+
+        @pl.when(near)
         def _():
-            ssend[k] = both.astype(BF16)
-            copy.start()
-
-        z_sends.append((b, copy))
-
-    down(0)
-    p0, p1 = (pl.ds(lo, size) for lo, size in parts)
-    arrived(hbuf.at[xnb, :, p0], rh.at[xnb, 0])
-    send(hbuf.at[xnb, :, p0], hbuf.at[xnb, :, p0], th.at[0, 2], rh.at[xnb, 0], (ynb, j))
-    pair(0)
-    arrived(hbuf.at[ynb, :, p0], rh.at[ynb, 0])
-    arrived(hbuf.at[ynb, :, p1], rh.at[ynb, 1])
-    send(hbuf.at[ynb, :, p1], hbuf.at[ynb, :, p1], th.at[1, 2], rh.at[ynb, 1], (xnb, j))
-    arrived(hbuf.at[xnb, :, p1], rh.at[xnb, 1])
-    down(1)
-    down(2)
-    pair(1)
-    pair(2)
-    arrived(hbuf.at[diag, :, p0], rh.at[diag, 0])
-    arrived(hbuf.at[diag, :, p1], rh.at[diag, 1])
-    down(3)
-    pair(3)
+            ssend[k, :, at] = qf[k, c, :, at].astype(BF16)
+            direct.start()
+
+        @pl.when(jnp.logical_and(away, outer))
+        def _():
+            ssend[k, :, at] = qf[k, c, :, at].astype(BF16)
+            passed.start()
+
+        away_sends.append((here, away, direct, joined))
+
+    def join(k, h):
+        b, at = blocks[k], halves[h]
+        _, away, _, joined = away_sends[2 * k + h]
+
+        @pl.when(jnp.logical_and(away, inner))
+        def _():
+            arrived(zpass.at[b, :, at], rpass.at[b, h])
+            ssend[k, :, at] = (qf[k, c, :, at] + zpass[b, :, at].astype(F32)).astype(BF16)
+            joined.start()
+
+    def hand_on(p):
+        cols = pl.ds(parts[p][0], parts[p][1])
+        src, to = ((xnb, ynb), (ynb, xnb))[p % 2]
+        arrived(hbuf.at[src, :, cols], rh.at[src, p])
+        send(hbuf.at[src, :, cols], hbuf.at[src, :, cols], th.at[p, 2], rh.at[src, p], (to, j))
+
+    def rest(p, src):
+        cols = pl.ds(parts[p][0], parts[p][1])
+        arrived(hbuf.at[src, :, cols], rh.at[src, p])
+
+    last = len(parts) - 1
+    down(0, 0)
+    hand_on(0)
+    down(0, 1)
+    pair(0, 0)
+    for p in range(1, last):
+        hand_on(p)
+    pair(0, 1)
+    hand_on(last)
+    for p in range(1, last + 1, 2):
+        rest(p, xnb)
+    down(1, 0)
+    down(1, 1)
+    pair(1, 0)
+    for p in range(0, last + 1, 2):
+        rest(p, ynb)
+    down(2, 0)
+    pair(1, 1)
+    join(0, 0)
+    join(0, 1)
+    down(2, 1)
+    pair(2, 0)
+    for p in range(last + 1):
+        rest(p, diag)
+    down(3, 0)
+    pair(2, 1)
+    down(3, 1)
+    pair(3, 0)
+    pair(3, 1)
+    for k in range(1, 4):
+        join(k, 0)
+        join(k, 1)
 
     first = j * (half_rows // R)
     mine = xbuf.reshape(xbuf.shape[0] * m, R, width)
     value = acc[...]
-    for step in range(1, chips):
-        slot = (z + step) % chips
-        arrived(zr.at[slot], rz.at[slot])
+    for slot in range(2):
+        for h in range(2):
+            arrived(zr.at[slot, :, halves[h]], rz.at[slot, h])
         value = value + zr[slot].astype(F32)
     acc[...] = value
     sums = []
@@ -316,15 +386,14 @@
     for other in (xnb, ynb, diag):
         arrived(call.at[other], rc.at[other])
         check = check + call[other]
-    chk_ref[...] = check / x_ref.shape[1]
+    chk_ref[...] = jnp.transpose(check / x_ref.shape[1])[0]
 
     for copy in sends:
         copy.wait_send()
-    for b, copy in z_sends:
-
-        @pl.when(b != z)
-        def _():
-            copy.wait_send()
+    for copy in inner_sends:
+        pl.when(inner)(copy.wait_send)
+    for here, _, copy, _ in away_sends:
+        pl.when(jnp.logical_not(here))(copy.wait_send)
 
 
 def on_plane(saved_input, keep_bits, norm_gain, gate_weight, up_weight, down_weight):
@@ -349,18 +418,18 @@
         pltpu.VMEM((n, TB, U), BF16),
         pltpu.VMEM((n, 2, out_rows, width), F32), pltpu.VMEM((n, 2, out_rows, width), BF16),
         pltpu.VMEM((n, out_rows, width), BF16), pltpu.VMEM((n, out_rows, width), BF16),
-        pltpu.VMEM((out_rows, width), F32), pltpu.VMEM((chips, out_rows, width), BF16),
+        pltpu.VMEM((out_rows, width), F32), pltpu.VMEM((2, out_rows, width), BF16), pltpu.VMEM((n, out_rows, width), BF16),
         pltpu.VMEM((out_rows, 128), F32), pltpu.VMEM((n, out_rows, 128), F32),
-        dma((3,)), dma((n, m)), dma((3,)), dma((n, chips - 1)), dma((n, chips)),
+        dma((3,)), dma((n, m)), dma((3,)), dma((n, 4)), dma((n, chips)),
         dma((m,)), dma((m - 1,)), dma((m,)), dma((m - 1,)),
-        dma((2, 6)), dma((2, 6)), dma((n, 2)), dma((2, 3)),
-        dma((n,)), dma((n,)), dma((chips,)), dma((n,)), dma((n,)), dma((3,)),
+        dma((COL_PARTS, 6)), dma((COL_PARTS, 6)), dma((n, COL_PARTS)), dma((COL_PARTS, 3)),
+        dma((n, 2)), dma((n, 2)), dma((2, 2)), dma((n, 2)), dma((n, 2)), dma((n,)), dma((3,)),
     ]
     layer_out, check = pl.pallas_call(
         fused,
         out_shape=(
             jax.ShapeDtypeStruct((out_rows, width), BF16),
-            jax.ShapeDtypeStruct((out_rows, 128), F32),
+            jax.ShapeDtypeStruct((out_rows,), F32),
         ),
         in_specs=[vmem, vmem, vmem, hbm, hbm, hbm],
         out_specs=(vmem, vmem),
@@ -368,8 +437,8 @@
         compiler_params=pltpu.CompilerParams(
             collective_id=0, has_side_effects=True, vmem_limit_bytes=60 * 1024 * 1024
         ),
-    )(saved_input, keep_bits, norm_gain.reshape(1, width), gate_weight, up_weight, down_weight)
-    return layer_out, check[:, 0]
+    )(saved_input, keep_bits, norm_gain, gate_weight, up_weight, down_weight)
+    return layer_out, check
 
 
 def solution(mesh):

time: 113 us -> 101 us (0.89)
  Pallas kernels: 107 us -> 97.3 us
  local copies, waits for them, and re-layouts: 4.34 us -> 2.8 us
    pallas_call x1, Pallas kernels: 107 us -> 97.3 us  [on_plane(): pl.pallas_call(fused, out_shape=(jax.ShapeDtypeStruct((out_rows, width),...]
    slice x1 -> x0, local copies, waits for them, and re-layouts: 1.38 us -> none  [on_plane(): return (layer_out, check[:, 0])]
    reshape x1 -> x0, local copies, waits for them, and re-layouts: 1.29 us -> none  [on_plane(): norm_gain.reshape(1, width)]
    unnamed x1 -> x2, local copies, waits for them, and re-layouts: 1.67 us -> 2.8 us
where the time goes in v2:
time: 101 us
  Pallas kernels  97.3 us (96%)
  local copies, waits for them, and re-layouts  2.8 us (3%)
    pallas_call x1, Pallas kernels, on_plane(): pl.pallas_call(fused, out_shape=(jax.ShapeDtypeStruct((out_rows, width),...  97.3 us
    unnamed x2, local copies, waits for them, and re-layouts  2.8 us

profile of v2, /device:TPU:0, one launch (start us, length us, event | category | flops | bytes accessed | tf_op | source)
XLA Modules:
  0.0 100.8 jit_solution(4334184457626852068)
XLA Ops:
  0.6 97.3 %shard_map.77 = (bf16[64,2048]{1,0:T(8,128)(2,1)}, f32[64]{0:T(128)}) custom-call(bf16[16,8192]{1,0:T(8,128)(2,1)} %x_ref.1, s32[16,448]{1,0:T(8,128)} %kb_ref.1, bf16[2048]{0:T(1024)(128)(2,1)} %gain_ref.1, bf16[2048,1792]{1,0:T(8,128)(2,1)} %wg_hbm.1, bf16[2048,1792]{1,0:T(8,128)(2,1)} %wu_hbm.1, bf16[1792,2048]{1,0:T(8,128)(2,1)} %wd_hbm.1), custom_call_target="tpu_custom_call" | custom-call | tf_op jit(solution)/shard_map/pallas_call | solution.py:428
  98.0 1.7 %copy.10 = bf16[64,2048]{1,0:T(8,128)(2,1)} copy(bf16[64,2048]{1,0:T(8,128)(2,1)} %get-tuple-element.4) | data formatting | bytes 524288
  99.6 1.1 %copy.11 = f32[64]{0:T(128)} copy(f32[64]{0:T(128)} %get-tuple-element.5) | data formatting | bytes 512
